TPU v7x, 32 devices: a whole 2x2x4 slice. The times are simulated.
32 devices in a mesh: row: 4 (over z), col: 8 (over y, x, core).
Axes of the slice: x: 2, y: 2, z: 4, core: 2. Of those that a mesh axis runs over, the one named last changes fastest.
Arguments:
- band_sites: float32 [2, 128], P(None, 'row'), may hold values from 0 to 1
- test_sites: float32 [2, 1024], P(None, 'col'), may hold values from 0 to 1
- band_factor: float32 [128, 128], P('row', 'col'), as said below
- prior_factor: float32 [128, 2048], P('row', 'col'), may hold values from -0.125 to 0.125
- prior_solution: float32 [2048, 1024], P('col', 'row'), may hold values from -6 to 6
- prior_covariance: float32 [1024, 1024], P('row', 'col'), may hold values from -4 to 4
Outputs:
- band_solution: float32 [128, 1024], P('row', 'col')
- covariance: float32 [1024, 1024], P('row', 'col')
Inputs may be any that keep to these rules, and one draw needn't show every extreme that they name: band_factor is lower triangular with diagonal entries in 1 to 2 and small entries below it.
All inputs are finite; a program needn't handle non-finite values.
Results may differ from a plain program's by a relative error of at most 0.00011.
Values sent between devices are 32-bit elements; how exact they have to be, the bound alone decides.
No kernel may reach another device: no remote copies, remote signals or barrier semaphores. Data moves between devices by JAX's collectives and lax.ppermute only.
A program may use at most 64 MiB of HBM per device.

v0:
```python
import jax
import jax.numpy as jnp
from jax import lax
from jax.sharding import PartitionSpec as P

length_scale = 0.3


def matern(band_sites, test_sites):
    delta_x = band_sites[0][:, None] - test_sites[0][None, :]
    delta_y = band_sites[1][:, None] - test_sites[1][None, :]
    scaled = jnp.sqrt(delta_x * delta_x + delta_y * delta_y + 1e-06) * (3.0**0.5 / length_scale)
    return (1.0 + scaled) * jnp.exp(-scaled)


def local(band_sites, test_sites, band_factor, prior_factor, prior_solution, prior_covariance):
    tile_rows = band_factor.shape[0]
    test_cols = test_sites.shape[1]
    row_count = lax.axis_size("row")
    my_row = lax.axis_index("row")
    cross = matern(band_sites, test_sites)
    partial_terms = lax.dot_general(
        lax.all_gather(prior_solution, "row", axis=1, tiled=True),
        prior_factor,
        (((0,), (1,)), ((), ())),
        precision=lax.Precision.HIGHEST,
        preferred_element_type=jnp.float32,
    )
    update = lax.psum_scatter(partial_terms, "col", scatter_dimension=0, tiled=True)
    remaining = cross - update.T
    factor_row = lax.all_gather(band_factor, "col", axis=1, tiled=True)
    whole_rest = lax.all_gather(remaining, "row", axis=0, tiled=True)
    whole_factor = lax.all_gather(factor_row, "row", axis=0, tiled=True)
    whole_solved = lax.linalg.triangular_solve(whole_factor, whole_rest, left_side=True, lower=True)
    collected = whole_solved.reshape(row_count, tile_rows, test_cols)
    band_solution = lax.dynamic_index_in_dim(collected, my_row, 0, keepdims=False)
    band_rows = lax.all_gather(band_solution, "col", axis=1, tiled=True)
    gram_sum = lax.psum_scatter(
        lax.dot_general(
            band_rows,
            band_solution,
            (((0,), (0,)), ((), ())),
            precision=lax.Precision.HIGHEST,
            preferred_element_type=jnp.float32,
        ),
        "row",
        scatter_dimension=0,
        tiled=True,
    )
    return (band_solution, prior_covariance - gram_sum)


def solution(mesh):
    placed = (
        P(None, "row"),
        P(None, "col"),
        P("row", "col"),
        P("row", "col"),
        P("col", "row"),
        P("row", "col"),
    )
    return jax.shard_map(
        local,
        mesh=mesh,
        in_specs=placed,
        out_specs=(P("row", "col"), P("row", "col")),
        check_vma=False,
    )
```

profile of v0, /device:TPU:0, one launch (start us, length us, event | category | flops | bytes accessed | tf_op | source)
XLA Modules:
  0.0 136.1 jit_solution(165506387914576891)
XLA Ops:
  7.2 0.0 copy-start
  7.2 0.0 all-gather.3.cloned.1.call-start
  7.2 0.7 all-gather.3.cloned.1.call-update
  7.9 0.0 copy-start.3
  7.9 0.0 reduce-scatter.3.cloned.1.call-start
  8.0 0.6 copy-done.3
  8.6 10.7 %all_gather.15 = f32[32,128]{0,1:T(8,128)S(1)} all-gather(f32[32,16]{0,1:T(8,128)S(1)} %copy-done.3), channel_id=1, replica_groups=mesh['row'=4,'col'=8] {'col'}, dimensions={1}, use_global_device_ids=true | all-gather | bytes 18432 | tf_op jit(solution)/shard_map/all_gather | solution.py:31
  19.3 0.1 copy.12
  19.4 14.0 %all_gather.16 = f32[128,128]{1,0:T(8,128)S(1)} all-gather(f32[32,128]{1,0:T(8,128)S(1)} %copy.12), channel_id=1, replica_groups=mesh['row'=4,'col'=8] {'row'}, dimensions={0}, use_global_device_ids=true | all-gather | bytes 81920 | tf_op jit(solution)/shard_map/all_gather | solution.py:33
  33.4 9.8 %custom-call.3 = f32[1,128,128]{1,2,0:T(8,128)S(1)} custom-call(f32[1,128,128]{2,1,0:T(8,128)S(1)} %select_bitcast_fusion), custom_call_target="InvertDiagBlocksLowerTriangular" | custom-call | tf_op jit(solution)/shard_map/triangular_solve | solution.py:34
  43.2 0.1 copy.13
  43.3 0.0 copy-start.4
  43.3 0.7 copy-done.4
  44.0 0.0 all-gather.3.cloned.1.call-done
  44.0 0.0 copy-done
  44.0 2.6 %fusion.4 = f32[1024,32]{0,1:T(8,128)} fusion(f32[256,1024]{1,0:T(8,128)} %all-gather.3.cloned.1.call-done, f32[32,256]{1,0:T(8,128)S(1)} %copy-done), kind=kOutput, calls=%fused_computation.12 | convolution fusion | flops 100663296 | bytes 1212416 | tf_op jit(solution)/shard_map/dot_general | solution.py:22
  46.6 0.0 copy-start.5
  46.6 0.0 reduce-scatter.3.cloned.1.call-update
  46.6 0.0 reduce-scatter.5.cloned.1.call-start
  46.7 0.6 copy-done.5
  47.3 33.4 %reduce-scatter.3.cloned.1.call-done = f32[128,32]{0,1:T(8,128)} async-done(((f32[1024,32]{0,1:T(8,128)}), f32[128,32]{0,1:T(8,128)}) %reduce-scatter.3.cloned.1.call-update) | async-done | bytes 16400 | tf_op jit(solution)/shard_map/reduce_scatter | solution.py:29
  80.7 0.8 bitcast_subtract_fusion
  81.5 13.3 %all_gather.18 = f32[128,128]{1,0:T(8,128)S(1)} all-gather(f32[32,128]{1,0:T(8,128)S(1)} %bitcast_subtract_fusion), channel_id=1, replica_groups=mesh['row'=4,'col'=8] {'row'}, dimensions={0}, use_global_device_ids=true | all-gather | bytes 81920 | tf_op jit(solution)/shard_map/all_gather | solution.py:32
  94.7 0.2 fusion.2
  95.0 0.0 copy-start.2
  95.0 9.3 %all-gather = f32[1,32,1024]{2,1,0:T(8,128)S(1)} all-gather(f32[1,32,128]{2,1,0:T(8,128)S(1)} %constant_dynamic-slice_fusion), channel_id=2, replica_groups=mesh['row'=4,'col'=8] {'col'}, dimensions={2}, use_global_device_ids=true | all-gather | bytes 147456 | tf_op jit(solution)/shard_map/all_gather | solution.py:37
  104.3 0.0 copy-done.2
  104.3 1.8 %fusion = f32[1024,128]{1,0:T(8,128)} fusion(f32[32,128]{1,0:T(8,128)S(1)} %fusion.9, f32[1,32,1024]{2,1,0:T(8,128)S(1)} %all-gather), kind=kOutput, calls=%fused_computation | convolution fusion | flops 50331648 | bytes 671744 | tf_op jit(solution)/shard_map/dot_general | solution.py:39
  106.0 0.0 copy-start.1
  106.0 0.0 reduce-scatter.5.cloned.1.call-update
  106.1 21.9 %reduce-scatter.5.cloned.1.call-done = f32[256,128]{1,0:T(8,128)} async-done(((f32[1024,128]{1,0:T(8,128)}), f32[256,128]{1,0:T(8,128)}) %reduce-scatter.5.cloned.1.call-update) | async-done | bytes 131088 | tf_op jit(solution)/shard_map/reduce_scatter | solution.py:38
  128.0 0.0 copy-done.1
  128.0 1.6 %sub.51 = f32[256,128]{1,0:T(8,128)} subtract(f32[256,128]{1,0:T(8,128)S(1)} %copy-done.1, f32[256,128]{1,0:T(8,128)} %reduce-scatter.5.cloned.1.call-done) | non-fusion elementwise | flops 32768 | bytes 393216 | tf_op jit(solution)/shard_map/sub | solution.py:50
  (5 shorter events, 0.0 us)
Async XLA Ops:
  7.2 36.8 %copy-start = (f32[32,256]{1,0:T(8,128)S(1)}, f32[32,256]{1,0:T(8,128)}, u32[]{:S(2)}) copy-start(f32[32,256]{1,0:T(8,128)} %param.9) | copy-start | bytes 98308
  7.2 36.8 %all-gather.3.cloned.1.call-start = ((), (), s32[]{:S(2)}) async-start(), calls=%async_computation.2 | async-start | bytes 1310720 | tf_op jit(solution)/shard_map/all_gather | solution.py:23
  7.9 0.7 copy-start.3
  7.9 72.7 %reduce-scatter.3.cloned.1.call-start = ((), (), s32[]{:S(2)}) async-start(), calls=%async_computation.3 | async-start | bytes 147456 | tf_op jit(solution)/shard_map/reduce_scatter | solution.py:29
  43.3 0.7 copy-start.4
  46.6 0.7 copy-start.5
  46.6 81.3 %reduce-scatter.5.cloned.1.call-start = ((), (), s32[]{:S(2)}) async-start(), calls=%async_computation.4 | async-start | bytes 655360 | tf_op jit(solution)/shard_map/reduce_scatter | solution.py:38
  95.0 9.3 %copy-start.2 = (f32[32,128]{1,0:T(8,128)}, f32[32,128]{1,0:T(8,128)S(1)}, u32[]{:S(2)}) copy-start(f32[32,128]{1,0:T(8,128)S(1)} %fusion.9) | copy-start | bytes 49156
  106.0 21.9 %copy-start.1 = (f32[256,128]{1,0:T(8,128)S(1)}, f32[256,128]{1,0:T(8,128)}, u32[]{:S(2)}) copy-start(f32[256,128]{1,0:T(8,128)} %param.11) | copy-start | bytes 393220
Sparse Core Ops, SparseCore 0:
  9.6 31.7 all-gather.2
  46.8 33.8 reduce-scatter.2
  106.2 21.7 reduce-scatter.4
where the time goes:
time: 136 us
  waiting for transfers between devices  56 us (41%)
  blocking collectives  47.2 us (35%)
  between operations  13.8 us (10%)
  other arithmetic  12.2 us (9%)
  matrix products  4.6 us (3%)
  local copies, waits for them, and re-layouts  2.12 us (2%)
    reduce_scatter x1, waiting for transfers between devices, local(): lax.psum_scatter(partial_terms, 'col', scatter_dimension=0, tiled=True)  33.4 us
    reduce_scatter x1, waiting for transfers between devices, local(): lax.psum_scatter(lax.dot_general(band_rows, band_solution, (((0,), (0,)),...  21.9 us
    all_gather x1, blocking collectives, local(): whole_factor = lax.all_gather(factor_row, 'row', axis=0, tiled=True)  14 us
    all_gather x1, blocking collectives, local(): whole_rest = lax.all_gather(remaining, 'row', axis=0, tiled=True)  13.3 us
    all_gather x1, blocking collectives, local(): factor_row = lax.all_gather(band_factor, 'col', axis=1, tiled=True)  10.7 us
    another operation x2, other arithmetic, local(): lax.linalg.triangular_solve(whole_factor, whole_rest, left_side=True, low...  9.82 us
    all_gather x1, blocking collectives, local(): band_rows = lax.all_gather(band_solution, 'col', axis=1, tiled=True)  9.25 us
  transfers between devices with their start and end apart: 3, of which 2 were waited for; matrix products, arithmetic and copies ran while one was open for 7% of the time, Pallas kernels for 0%

commit v1 on v0

--- a/solution.py
+++ b/solution.py
@@ -29,8 +29,11 @@
     update = lax.psum_scatter(partial_terms, "col", scatter_dimension=0, tiled=True)
     remaining = cross - update.T
     factor_row = lax.all_gather(band_factor, "col", axis=1, tiled=True)
-    whole_rest = lax.all_gather(remaining, "row", axis=0, tiled=True)
-    whole_factor = lax.all_gather(factor_row, "row", axis=0, tiled=True)
+    whole_rest, whole_factor = jnp.split(
+        lax.all_gather(jnp.concatenate([remaining, factor_row], axis=1), "row", axis=0, tiled=True),
+        [remaining.shape[1]],
+        axis=1,
+    )
     whole_solved = lax.linalg.triangular_solve(whole_factor, whole_rest, left_side=True, lower=True)
     collected = whole_solved.reshape(row_count, tile_rows, test_cols)
     band_solution = lax.dynamic_index_in_dim(collected, my_row, 0, keepdims=False)

time: 136 us -> 143 us (1.051)
  waiting for transfers between devices: 56 us -> 76.1 us
  blocking collectives: 47.2 us -> 33.5 us
    all_gather x1, waiting for transfers between devices: 0.01 us -> 20.2 us  [local(): lax.all_gather(prior_solution, 'row', axis=1, tiled=True)]
    all_gather x2 -> x1, blocking collectives: 27.3 us -> 13.4 us  [local(): lax.all_gather(jnp.concatenate([remaining, factor_row], axis=1), 'row', a...]
  transfers between devices with their start and end apart: 3 -> 3, of which waited for: 2 -> 3; matrix products, arithmetic and copies ran while one was open for 7% -> 0% of each run, Pallas kernels for 0% -> 0%
where the time goes in v1:
time: 143 us; the launch traced here: 142 us
  waiting for transfers between devices  76.1 us (53%)
  blocking collectives  33.5 us (23%)
  between operations  13.8 us (10%)
  other arithmetic  12.2 us (9%)
  matrix products  4.6 us (3%)
  local copies, waits for them, and re-layouts  2.14 us (1%)
    reduce_scatter x1, waiting for transfers between devices, local(): lax.psum_scatter(partial_terms, 'col', scatter_dimension=0, tiled=True)  33.2 us
    reduce_scatter x1, waiting for transfers between devices, local(): lax.psum_scatter(lax.dot_general(band_rows, band_solution, (((0,), (0,)),...  21.9 us
    all_gather x1, waiting for transfers between devices, local(): lax.all_gather(prior_solution, 'row', axis=1, tiled=True)  20.2 us
    all_gather x1, blocking collectives, local(): lax.all_gather(jnp.concatenate([remaining, factor_row], axis=1), 'row', a...  13.4 us
    all_gather x1, blocking collectives, local(): factor_row = lax.all_gather(band_factor, 'col', axis=1, tiled=True)  10.7 us
    another operation x2, other arithmetic, local(): lax.linalg.triangular_solve(whole_factor, whole_rest, left_side=True, low...  9.82 us
    all_gather x1, blocking collectives, local(): band_rows = lax.all_gather(band_solution, 'col', axis=1, tiled=True)  9.36 us
  transfers between devices with their start and end apart: 3, of which 3 were waited for; matrix products, arithmetic and copies ran while one was open for 0% of the time, Pallas kernels for 0%

profile of v1, /device:TPU:0, one launch (start us, length us, event | category | flops | bytes accessed | tf_op | source)
XLA Modules:
  0.0 142.4 jit_solution(15394842557910586646)
XLA Ops:
  7.2 0.0 copy-start
  7.2 0.0 all-gather.3.cloned.1.call-start
  7.2 0.7 all-gather.3.cloned.1.call-update
  7.9 0.0 copy-start.3
  7.9 0.0 reduce-scatter.3.cloned.1.call-start
  8.0 0.6 copy-done.3
  8.6 10.7 %all_gather.13 = f32[32,128]{0,1:T(8,128)S(1)} all-gather(f32[32,16]{0,1:T(8,128)S(1)} %copy-done.3), channel_id=1, replica_groups=mesh['row'=4,'col'=8] {'col'}, dimensions={1}, use_global_device_ids=true | all-gather | bytes 18432 | tf_op jit(solution)/shard_map/all_gather | solution.py:31
  19.3 0.1 copy.12
  19.4 0.0 copy-start.4
  19.4 0.7 copy-done.4
  20.1 20.2 %all-gather.3.cloned.1.call-done = f32[256,1024]{1,0:T(8,128)} async-done(((f32[256,256]{1,0:T(8,128)}), f32[256,1024]{1,0:T(8,128)}) %all-gather.3.cloned.1.call-update) | async-done | bytes 1048592 | tf_op jit(solution)/shard_map/all_gather | solution.py:23
  40.3 0.0 copy-done
  40.3 2.6 %fusion.4 = f32[1024,32]{0,1:T(8,128)} fusion(f32[256,1024]{1,0:T(8,128)} %all-gather.3.cloned.1.call-done, f32[32,256]{1,0:T(8,128)S(1)} %copy-done), kind=kOutput, calls=%fused_computation.14 | convolution fusion | flops 100663296 | bytes 1212416 | tf_op jit(solution)/shard_map/dot_general | solution.py:22
  42.9 0.0 copy-start.5
  42.9 0.0 reduce-scatter.3.cloned.1.call-update
  42.9 0.0 reduce-scatter.5.cloned.1.call-start
  43.0 0.6 copy-done.5
  43.6 33.2 %reduce-scatter.3.cloned.1.call-done = f32[128,32]{0,1:T(8,128)} async-done(((f32[1024,32]{0,1:T(8,128)}), f32[128,32]{0,1:T(8,128)}) %reduce-scatter.3.cloned.1.call-update) | async-done | bytes 16400 | tf_op jit(solution)/shard_map/reduce_scatter | solution.py:29
  76.8 0.8 bitcast_subtract_fusion
  77.7 13.4 %all_gather.14 = f32[128,256]{1,0:T(8,128)S(1)} all-gather(f32[32,256]{1,0:T(8,128)S(1)} %pad_maximum_fusion), channel_id=1, replica_groups=mesh['row'=4,'col'=8] {'row'}, dimensions={0}, use_global_device_ids=true | all-gather | bytes 163840 | tf_op jit(solution)/shard_map/all_gather | solution.py:33
  91.1 9.8 %custom-call.3 = f32[1,128,128]{1,2,0:T(8,128)S(1)} custom-call(f32[1,128,128]{2,1,0:T(8,128)S(1)} %fusion.3), custom_call_target="InvertDiagBlocksLowerTriangular" | custom-call | tf_op jit(solution)/shard_map/triangular_solve | solution.py:37
  100.9 0.1 copy.13
  101.0 0.2 fusion.2
  101.2 0.0 copy-start.2
  101.3 9.4 %all-gather = f32[1,32,1024]{2,1,0:T(8,128)S(1)} all-gather(f32[1,32,128]{2,1,0:T(8,128)S(1)} %constant_dynamic-slice_fusion), channel_id=2, replica_groups=mesh['row'=4,'col'=8] {'col'}, dimensions={2}, use_global_device_ids=true | all-gather | bytes 147456 | tf_op jit(solution)/shard_map/all_gather | solution.py:40
  110.6 0.0 copy-done.2
  110.6 1.8 %fusion = f32[1024,128]{1,0:T(8,128)} fusion(f32[32,128]{1,0:T(8,128)S(1)} %fusion.9, f32[1,32,1024]{2,1,0:T(8,128)S(1)} %all-gather), kind=kOutput, calls=%fused_computation | convolution fusion | flops 50331648 | bytes 671744 | tf_op jit(solution)/shard_map/dot_general | solution.py:42
  112.4 0.0 copy-start.1
  112.4 0.0 reduce-scatter.5.cloned.1.call-update
  112.5 21.9 %reduce-scatter.5.cloned.1.call-done = f32[256,128]{1,0:T(8,128)} async-done(((f32[1024,128]{1,0:T(8,128)}), f32[256,128]{1,0:T(8,128)}) %reduce-scatter.5.cloned.1.call-update) | async-done | bytes 131088 | tf_op jit(solution)/shard_map/reduce_scatter | solution.py:41
  134.3 0.0 copy-done.1
  134.3 1.6 %sub.51 = f32[256,128]{1,0:T(8,128)} subtract(f32[256,128]{1,0:T(8,128)S(1)} %copy-done.1, f32[256,128]{1,0:T(8,128)} %reduce-scatter.5.cloned.1.call-done) | non-fusion elementwise | flops 32768 | bytes 393216 | tf_op jit(solution)/shard_map/sub | solution.py:53
  (6 shorter events, 0.0 us)
Async XLA Ops:
  7.2 33.1 %copy-start = (f32[32,256]{1,0:T(8,128)S(1)}, f32[32,256]{1,0:T(8,128)}, u32[]{:S(2)}) copy-start(f32[32,256]{1,0:T(8,128)} %param.9) | copy-start | bytes 98308
  7.2 33.1 %all-gather.3.cloned.1.call-start = ((), (), s32[]{:S(2)}) async-start(), calls=%async_computation.2 | async-start | bytes 1310720 | tf_op jit(solution)/shard_map/all_gather | solution.py:23
  7.9 0.7 copy-start.3
  7.9 68.9 %reduce-scatter.3.cloned.1.call-start = ((), (), s32[]{:S(2)}) async-start(), calls=%async_computation.3 | async-start | bytes 147456 | tf_op jit(solution)/shard_map/reduce_scatter | solution.py:29
  19.4 0.7 copy-start.4
  42.9 0.7 copy-start.5
  42.9 91.4 %reduce-scatter.5.cloned.1.call-start = ((), (), s32[]{:S(2)}) async-start(), calls=%async_computation.4 | async-start | bytes 655360 | tf_op jit(solution)/shard_map/reduce_scatter | solution.py:41
  101.2 9.4 %copy-start.2 = (f32[32,128]{1,0:T(8,128)}, f32[32,128]{1,0:T(8,128)S(1)}, u32[]{:S(2)}) copy-start(f32[32,128]{1,0:T(8,128)S(1)} %fusion.9) | copy-start | bytes 49156
  112.4 21.9 %copy-start.1 = (f32[256,128]{1,0:T(8,128)S(1)}, f32[256,128]{1,0:T(8,128)}, u32[]{:S(2)}) copy-start(f32[256,128]{1,0:T(8,128)} %param.11) | copy-start | bytes 393220
Sparse Core Ops, SparseCore 0:
  9.6 30.6 all-gather.2
  43.9 32.9 reduce-scatter.2
  112.6 21.7 reduce-scatter.4
